TPU v7x, 32 devices: a whole 2x2x4 slice. The times are simulated.
32 devices in a mesh: gx: 4 (over y, x), gy: 8 (over z, core).
Axes of the slice: x: 2, y: 2, z: 4, core: 2. Of those that a mesh axis runs over, the one named last changes fastest.
Arguments:
- features: bfloat16 [32, 32, 64, 128], P(None, 'gx', 'gy'), may hold values from -6 to 6
- weight_two: bfloat16 [27, 32, 32], replicated, may hold values from -0.21875 to 0.21875
- bias_two: float32 [32], replicated, may hold values from -3 to 3
- weight_three: bfloat16 [27, 64, 32], replicated, may hold values from -0.21875 to 0.21875
- bias_three: float32 [64], replicated, may hold values from -3 to 3
- weight_four: bfloat16 [27, 128, 64], replicated, may hold values from -0.25 to 0.25
- bias_four: float32 [128], replicated, may hold values from -3 to 3
Outputs:
- level_two: bfloat16 [32, 32, 64, 128], P(None, 'gx', 'gy')
- level_three: bfloat16 [64, 16, 32, 64], P(None, 'gx', 'gy')
- bottleneck: bfloat16 [128, 8, 16, 32], P(None, None, None, 'gy')
All inputs are finite; a program needn't handle non-finite values.
Results may differ from a plain program's by a relative error of at most 0.0085.
Values may be sent and summed in bfloat16 or wider, within the bound.
No kernel may reach another device: no remote copies, remote signals or barrier semaphores. Data moves between devices by JAX's collectives and lax.ppermute only.
A program may use at most 64 MiB of HBM per device.

v0:
```python
import jax
import jax.numpy as jnp
from jax import lax
from jax.sharding import PartitionSpec as P


def extended(cells, sides, width):
    for axis, dim in sides:
        count = lax.axis_size(axis)
        head = lax.slice_in_dim(cells, 0, width, axis=dim)
        tail = lax.slice_in_dim(cells, cells.shape[dim] - width, cells.shape[dim], axis=dim)
        cells = jnp.concatenate(
            [
                lax.ppermute(tail, axis, [(i, (i + 1) % count) for i in range(count)]),
                cells,
                lax.ppermute(head, axis, [((i + 1) % count, i) for i in range(count)]),
            ],
            axis=dim,
        )
    return cells


def wrap_axis(source, axis):
    first = lax.slice_in_dim(source, 0, 1, axis=axis)
    final = lax.slice_in_dim(source, source.shape[axis] - 1, source.shape[axis], axis=axis)
    return jnp.concatenate([final, source, first], axis=axis)


def convolve(padded, weights, bias_values):
    in_channels = padded.shape[0]
    extent_x = padded.shape[1] - 2
    extent_y = padded.shape[2] - 2
    extent_z = padded.shape[3] - 2
    out_channels = weights.shape[1]
    running = jnp.zeros((out_channels, extent_x * extent_y * extent_z), jnp.float32)
    for offset_x in range(3):
        for offset_y in range(3):
            stacked = jnp.concatenate(
                [
                    padded[
                        :,
                        offset_x : offset_x + extent_x,
                        offset_y : offset_y + extent_y,
                        offset_z : offset_z + extent_z,
                    ]
                    for offset_z in range(3)
                ],
                axis=0,
            ).reshape(3 * in_channels, -1)
            first_row = offset_x * 9 + offset_y * 3
            mixing = (
                weights[first_row : first_row + 3]
                .transpose(1, 0, 2)
                .reshape(out_channels, 3 * in_channels)
            )
            running = running + jnp.dot(mixing, stacked, preferred_element_type=jnp.float32)
    result = running + bias_values[:, None]
    result = jax.nn.leaky_relu(result, 0.1).astype(jnp.bfloat16)
    return result.reshape(out_channels, extent_x, extent_y, extent_z)


def average_pool(source):
    channels, extent_x, extent_y, extent_z = source.shape
    blocks = source.astype(jnp.float32).reshape(
        channels, extent_x // 2, 2, extent_y // 2, 2, extent_z // 2, 2
    )
    return blocks.mean(axis=(2, 4, 6)).astype(jnp.bfloat16)


def shards(features, weight_two, bias_two, weight_three, bias_three, weight_four, bias_four):
    rimmed = extended(features, (("gx", 1), ("gy", 2)), 1)
    level_two = convolve(wrap_axis(rimmed, 3), weight_two, bias_two)
    pooled = average_pool(level_two)
    rimmed_three = extended(pooled, (("gx", 1), ("gy", 2)), 1)
    level_three = convolve(wrap_axis(rimmed_three, 3), weight_three, bias_three)
    coarse = average_pool(level_three)
    pieces = lax.all_to_all(coarse, "gy", split_axis=3, concat_axis=2, tiled=True)
    slab_rows = lax.all_gather(pieces, "gx", axis=1, tiled=True)
    deepened = extended(slab_rows, (("gy", 3),), 1)
    padded = wrap_axis(wrap_axis(deepened, 1), 2)
    bottleneck = convolve(padded, weight_four, bias_four)
    return (level_two, level_three, bottleneck)


def solution(mesh):
    return jax.shard_map(
        shards,
        mesh=mesh,
        in_specs=(P(None, "gx", "gy", None), P(), P(), P(), P(), P(), P()),
        out_specs=(P(None, "gx", "gy", None), P(None, "gx", "gy", None), P(None, None, None, "gy")),
        check_vma=False,
    )
```

profile of v0, /device:TPU:0, one launch (start us, length us, event | category | flops | bytes accessed | tf_op | source)
XLA Modules:
  0.0 100.0 jit_solution(3070848087950724654)
XLA Ops:
  0.6 1.5 %copy.174 = bf16[32,8,8,128]{3,0,2,1:T(8,128)(2,1)S(1)} copy(bf16[32,8,8,128]{3,2,1,0:T(8,128)(2,1)} %param.7) | data formatting | bytes 1048576 | tf_op args[0]
  2.1 3.0 %collective-permute-start = (bf16[32,1,8,128]{3,0,2,1:T(8,128)(2,1)S(1)}, bf16[32,1,8,128]{3,0,2,1:T(8,128)(2,1)S(1)}, u32[]{:S(2)}, u32[]{:S(2)}) collective-permute-start(bf16[32,1,8,128]{3,0,2,1:T(8,128)(2,1)S(1)} %get-tuple-element.57), channel_id=1, source_target_pairs={{0,8},{8,16},{16,24},{24,0},{1,9},{9,17},{17,25},{25,1},{2,10},{10... | collective-permute-start | bytes 196616 | tf_op jit(solution)/shard_map/ppermute | solution.py:14
  5.1 1.0 %collective-permute-start.1 = (bf16[32,1,8,128]{3,0,2,1:T(8,128)(2,1)S(1)}, bf16[32,1,8,128]{3,0,2,1:T(8,128)(2,1)S(1)}, u32[]{:S(2)}, u32[]{:S(2)}) collective-permute-start(bf16[32,1,8,128]{3,0,2,1:T(8,128)(2,1)S(1)} %get-tuple-element.56), channel_id=1, source_target_pairs={{8,0},{16,8},{24,16},{0,24},{9,1},{17,9},{25,17},{1,25},{10,2},{18... | collective-permute-start | bytes 196616 | tf_op jit(solution)/shard_map/ppermute | solution.py:16
  6.2 2.3 %collective-permute-done = bf16[32,1,8,128]{3,0,2,1:T(8,128)(2,1)S(1)} collective-permute-done((bf16[32,1,8,128]{3,0,2,1:T(8,128)(2,1)S(1)}, bf16[32,1,8,128]{3,0,2,1:T(8,128)(2,1)S(1)}, u32[]{:S(2)}, u32[]{:S(2)}) %collective-permute-start) | collective-permute-done | bytes 65568 | tf_op jit(solution)/shard_map/ppermute | solution.py:14
  8.8 1.0 %collective-permute-done.1 = bf16[32,1,8,128]{3,0,2,1:T(8,128)(2,1)S(1)} collective-permute-done((bf16[32,1,8,128]{3,0,2,1:T(8,128)(2,1)S(1)}, bf16[32,1,8,128]{3,0,2,1:T(8,128)(2,1)S(1)}, u32[]{:S(2)}, u32[]{:S(2)}) %collective-permute-start.1) | collective-permute-done | bytes 65568 | tf_op jit(solution)/shard_map/ppermute | solution.py:16
  9.9 2.2 %collective-permute-start.3 = (bf16[32,10,1,128]{3,0,2,1:T(8,128)(2,1)S(1)}, bf16[32,10,1,128]{3,0,2,1:T(8,128)(2,1)S(1)}, u32[]{:S(2)}, u32[]{:S(2)}) collective-permute-start(bf16[32,10,1,128]{3,0,2,1:T(8,128)(2,1)S(1)} %get-tuple-element.52), channel_id=1, source_target_pairs={{1,0},{2,1},{3,2},{4,3},{5,4},{6,5},{7,6},{0,7},{9,8},{10,9},{11,1... | collective-permute-start | bytes 245768 | tf_op jit(solution)/shard_map/ppermute | solution.py:16
  13.2 1.0 %collective-permute-done.3 = bf16[32,10,1,128]{3,0,2,1:T(8,128)(2,1)S(1)} collective-permute-done((bf16[32,10,1,128]{3,0,2,1:T(8,128)(2,1)S(1)}, bf16[32,10,1,128]{3,0,2,1:T(8,128)(2,1)S(1)}, u32[]{:S(2)}, u32[]{:S(2)}) %collective-permute-start.3) | collective-permute-done | bytes 81952 | tf_op jit(solution)/shard_map/ppermute | solution.py:16
  14.2 3.6 %collective-permute-done.2 = bf16[32,10,1,128]{3,0,2,1:T(8,128)(2,1)S(1)} collective-permute-done((bf16[32,10,1,128]{3,0,2,1:T(8,128)(2,1)S(1)}, bf16[32,10,1,128]{3,0,2,1:T(8,128)(2,1)S(1)}, u32[]{:S(2)}, u32[]{:S(2)}) %collective-permute-start.2) | collective-permute-done | bytes 81952 | tf_op jit(solution)/shard_map/ppermute | solution.py:14
  18.2 1.7 %maximum_maximum_fusion = (bf16[32,10,10,129]{3,0,2,1:T(8,128)(2,1)S(1)}, bf16[32,10,10,129]{3,0,2,1:T(8,128)(2,1)S(1)}) fusion(bf16[32,10,1,128]{3,0,2,1:T(8,128)(2,1)S(1)} %collective-permute-done.3, bf16[32,10,8,128]{3,0,2,1:T(8,128)(2,1)S(1)} %constant_dynamic-update-slice_fusion, bf16[32,10,1,128]{3,0,2,1:T(8,128)(2,1)S(1)} %collective-permute-done.2, ...), kind=kLoop, calls=%fused_computation.11 | loop fusion | flops 6604800 | bytes 2483200 | tf_op jit(solution)/shard_map/concatenate | solution.py:26
  19.9 2.8 %fusion.60 = (bf16[32,8,8,128]{3,0,2,1:T(8,128)(2,1)S(1)}, bf16[32,8,8,128]{3,0,2,1:T(8,128)(2,1)S(1)}, bf16[32,8,8,128]{3,0,2,1:T(8,128)(2,1)S(1)}, bf16[32,8,8...) fusion(bf16[32,10,10,129]{3,0,2,1:T(8,128)(2,1)S(1)} %get-tuple, ...), kind=kLoop, calls=%fused_computation.164 | loop fusion | bytes 18874368 | tf_op jit(solution)/shard_map/slice | solution.py:40
  30.0 1.1 %fusion.18 = f32[8192,32]{0,1:T(8,128)S(1)} fusion(bf16[32,96]{1,0:T(8,128)(2,1)S(1)} %reshape.189, bf16[12,8,64,128]{3,2,1,0:T(8,128)(2,1)S(1)} %bitcast.226), kind=kOutput, calls=%fused_computation.29 | convolution fusion | flops 50331648 | bytes 2627584 | tf_op jit(solution)/shard_map/dot_general | solution.py:56
  31.1 1.1 %convolution_add_fusion.7 = f32[8192,32]{0,1:T(8,128)S(1)} fusion(f32[8192,32]{0,1:T(8,128)S(1)} %fusion.18, bf16[32,96]{1,0:T(8,128)(2,1)S(1)} %reshape.191, bf16[12,8,64,128]{3,2,1,0:T(8,128)(2,1)S(1)} %bitcast.227), kind=kOutput, calls=%fused_computation.9 | convolution fusion | flops 50593792 | bytes 3676160 | tf_op jit(solution)/shard_map/dot_general | solution.py:56
  32.2 1.1 %convolution_add_fusion.6 = f32[8192,32]{0,1:T(8,128)S(1)} fusion(f32[8192,32]{0,1:T(8,128)S(1)} %convolution_add_fusion.7, bf16[32,96]{1,0:T(8,128)(2,1)S(1)} %reshape.193, bf16[12,8,64,128]{3,2,1,0:T(8,128)(2,1)S(1)} %bitcast.228), kind=kOutput, calls=%fused_computation.8 | convolution fusion | flops 50593792 | bytes 3676160 | tf_op jit(solution)/shard_map/dot_general | solution.py:56
  33.4 1.1 %convolution_add_fusion.5 = f32[8192,32]{0,1:T(8,128)S(1)} fusion(f32[8192,32]{0,1:T(8,128)S(1)} %convolution_add_fusion.6, bf16[32,96]{1,0:T(8,128)(2,1)S(1)} %reshape.195, bf16[12,8,64,128]{3,2,1,0:T(8,128)(2,1)S(1)} %bitcast.230), kind=kOutput, calls=%fused_computation.7 | convolution fusion | flops 50593792 | bytes 3676160 | tf_op jit(solution)/shard_map/dot_general | solution.py:56
  34.5 1.1 %convolution_add_fusion.4 = f32[8192,32]{0,1:T(8,128)S(1)} fusion(f32[8192,32]{0,1:T(8,128)S(1)} %convolution_add_fusion.5, bf16[32,96]{1,0:T(8,128)(2,1)S(1)} %reshape.197, bf16[12,8,64,128]{3,2,1,0:T(8,128)(2,1)S(1)} %bitcast.229), kind=kOutput, calls=%fused_computation.6 | convolution fusion | flops 50593792 | bytes 3676160 | tf_op jit(solution)/shard_map/dot_general | solution.py:56
  35.6 1.1 %convolution_add_fusion.3 = f32[8192,32]{0,1:T(8,128)S(1)} fusion(f32[8192,32]{0,1:T(8,128)S(1)} %convolution_add_fusion.4, bf16[32,96]{1,0:T(8,128)(2,1)S(1)} %reshape.199, bf16[12,8,64,128]{3,2,1,0:T(8,128)(2,1)S(1)} %bitcast.231), kind=kOutput, calls=%fused_computation.5 | convolution fusion | flops 50593792 | bytes 3676160 | tf_op jit(solution)/shard_map/dot_general | solution.py:56
  36.7 1.1 %convolution_add_fusion.2 = f32[8192,32]{0,1:T(8,128)S(1)} fusion(f32[8192,32]{0,1:T(8,128)S(1)} %convolution_add_fusion.3, bf16[32,96]{1,0:T(8,128)(2,1)S(1)} %reshape.201, bf16[12,8,64,128]{3,2,1,0:T(8,128)(2,1)S(1)} %bitcast.233), kind=kOutput, calls=%fused_computation.4 | convolution fusion | flops 50593792 | bytes 3676160 | tf_op jit(solution)/shard_map/dot_general | solution.py:56
  37.9 1.1 %convolution_add_fusion.1 = f32[8192,32]{0,1:T(8,128)S(1)} fusion(f32[8192,32]{0,1:T(8,128)S(1)} %convolution_add_fusion.2, bf16[32,96]{1,0:T(8,128)(2,1)S(1)} %reshape.203, bf16[12,8,64,128]{3,2,1,0:T(8,128)(2,1)S(1)} %bitcast.232), kind=kOutput, calls=%fused_computation.3 | convolution fusion | flops 50593792 | bytes 3676160 | tf_op jit(solution)/shard_map/dot_general | solution.py:56
  39.0 1.1 %fusion.31 = bf16[32,8192]{1,0:T(8,128)(2,1)S(1)} fusion(f32[8192,32]{0,1:T(8,128)S(1)} %convolution_add_fusion.1, bf16[32,96]{1,0:T(8,128)(2,1)S(1)} %reshape.205, bf16[12,8,64,128]{3,2,1,0:T(8,128)(2,1)S(1)} %bitcast.234, f32[32]{0:T(128)S(1)} %copy-done.13), kind=kOutput, calls=%fused_computation.49 | convolution fusion | flops 51904512 | bytes 3152000 | tf_op jit(solution)/shard_map/dot_general | solution.py:56
  40.1 2.4 %copy.198 = f32[32,8192]{0,1:T(8,128)} copy(bf16[32,8192]{1,0:T(8,128)(2,1)S(1)} %fusion.31) | data formatting | bytes 1572864 | tf_op jit(solution)/shard_map/convert_element_type | solution.py:64
  42.5 4.8 %reduce_sum.18 = f32[32,4,4,64]{0,3,2,1:T(8,128)S(1)} reduce(f32[32,4,2,4,2,64,2]{0,6,5,4,3,2,1:T(2,128)} %bitcast.225, f32[]{:T(128)} %constant.6.clone.1), dimensions={2,4,6}, to_apply=%region_0.1 | reduce | flops 229376 | bytes 1179652 | tf_op jit(solution)/shard_map/reduce_sum | solution.py:67
  47.4 2.1 %collective-permute-start.5 = (bf16[32,1,4,64]{0,3,2,1:T(8,128)(2,1)S(1)}, bf16[32,1,4,64]{0,3,2,1:T(8,128)(2,1)S(1)}, u32[]{:S(2)}, u32[]{:S(2)}) collective-permute-start(bf16[32,1,4,64]{0,3,2,1:T(8,128)(2,1)S(1)} %get-tuple-element.99), channel_id=1, source_target_pairs={{8,0},{16,8},{24,16},{0,24},{9,1},{17,9},{25,17},{1,25},{10,2},{18... | collective-permute-start | bytes 49160 | tf_op jit(solution)/shard_map/ppermute | solution.py:16
  49.6 2.2 %collective-permute-done.5 = bf16[32,1,4,64]{0,3,2,1:T(8,128)(2,1)S(1)} collective-permute-done((bf16[32,1,4,64]{0,3,2,1:T(8,128)(2,1)S(1)}, bf16[32,1,4,64]{0,3,2,1:T(8,128)(2,1)S(1)}, u32[]{:S(2)}, u32[]{:S(2)}) %collective-permute-start.5) | collective-permute-done | bytes 16416 | tf_op jit(solution)/shard_map/ppermute | solution.py:16
  51.8 2.9 %collective-permute-done.4 = bf16[32,1,4,64]{0,3,2,1:T(8,128)(2,1)S(1)} collective-permute-done((bf16[32,1,4,64]{0,3,2,1:T(8,128)(2,1)S(1)}, bf16[32,1,4,64]{0,3,2,1:T(8,128)(2,1)S(1)}, u32[]{:S(2)}, u32[]{:S(2)}) %collective-permute-start.4) | collective-permute-done | bytes 16416 | tf_op jit(solution)/shard_map/ppermute | solution.py:14
  55.3 2.5 %collective-permute-done.7 = bf16[32,6,1,64]{0,3,2,1:T(8,128)(2,1)S(1)} collective-permute-done((bf16[32,6,1,64]{0,3,2,1:T(8,128)(2,1)S(1)}, bf16[32,6,1,64]{0,3,2,1:T(8,128)(2,1)S(1)}, u32[]{:S(2)}, u32[]{:S(2)}) %collective-permute-start.7) | collective-permute-done | bytes 24608 | tf_op jit(solution)/shard_map/ppermute | solution.py:16
  57.8 2.9 %collective-permute-done.6 = bf16[32,6,1,64]{0,3,2,1:T(8,128)(2,1)S(1)} collective-permute-done((bf16[32,6,1,64]{0,3,2,1:T(8,128)(2,1)S(1)}, bf16[32,6,1,64]{0,3,2,1:T(8,128)(2,1)S(1)}, u32[]{:S(2)}, u32[]{:S(2)}) %collective-permute-start.6) | collective-permute-done | bytes 24608 | tf_op jit(solution)/shard_map/ppermute | solution.py:14
  67.9 8.0 %all_to_all.18 = bf16[8,2,512]{2,1,0:T(2,128)(2,1)S(1)} all-to-all(bf16[8,2,512]{2,1,0:T(2,128)(2,1)S(1)} %reshape.247), channel_id=1, replica_groups=mesh['gx'=4,'gy'=8] {'gy'}, dimensions={0} | all-to-all | bytes 32768 | tf_op jit(solution)/shard_map/all_to_all | solution.py:77
  76.0 8.5 %all_gather.3 = bf16[64,8,16,4]{0,2,3,1:T(8,128)(2,1)S(1)} all-gather(bf16[64,2,16,4]{0,2,3,1:T(8,128)(2,1)S(1)} %bitcast.257), channel_id=1, replica_groups=mesh['gx'=4,'gy'=8] {'gx'}, dimensions={1}, use_global_device_ids=true | all-gather | bytes 81920 | tf_op jit(solution)/shard_map/all_gather | solution.py:78
  85.3 0.9 copy.221
  86.2 0.9 reshape.225
  87.1 3.5 %collective-permute-start.9 = (bf16[64,8,16,1]{0,2,3,1:T(8,128)(2,1)S(1)}, bf16[64,8,16,1]{0,2,3,1:T(8,128)(2,1)S(1)}, u32[]{:S(2)}, u32[]{:S(2)}) collective-permute-start(bf16[64,8,16,1]{0,2,3,1:T(8,128)(2,1)S(1)} %get-tuple-element.130), channel_id=1, source_target_pairs={{1,0},{2,1},{3,2},{4,3},{5,4},{6,5},{7,6},{0,7},{9,8},{10,9},{11,1... | collective-permute-start | bytes 49160 | tf_op jit(solution)/shard_map/ppermute | solution.py:16
  90.7 1.6 %collective-permute-done.9 = bf16[64,8,16,1]{0,2,3,1:T(8,128)(2,1)S(1)} collective-permute-done((bf16[64,8,16,1]{0,2,3,1:T(8,128)(2,1)S(1)}, bf16[64,8,16,1]{0,2,3,1:T(8,128)(2,1)S(1)}, u32[]{:S(2)}, u32[]{:S(2)}) %collective-permute-start.9) | collective-permute-done | bytes 16416 | tf_op jit(solution)/shard_map/ppermute | solution.py:16
  (156 shorter events, 25.2 us)
Async XLA Ops:
  0.6 7.8 %copy-start = (bf16[32,8,8,128]{3,2,1,0:T(8,128)(2,1)S(1)}, bf16[32,8,8,128]{3,2,1,0:T(8,128)(2,1)}, u32[]{:S(2)}) copy-start(bf16[32,8,8,128]{3,2,1,0:T(8,128)(2,1)} %param.7) | copy-start | bytes 1572868
  0.6 11.5 %copy-start.2 = (bf16[27,32,32]{2,1,0:T(8,128)(2,1)S(1)}, bf16[27,32,32]{2,1,0:T(8,128)(2,1)}, u32[]{:S(2)}) copy-start(bf16[27,32,32]{2,1,0:T(8,128)(2,1)} %param.8) | copy-start | bytes 165892
  2.1 6.3 %collective-permute-start = (bf16[32,1,8,128]{3,0,2,1:T(8,128)(2,1)S(1)}, bf16[32,1,8,128]{3,0,2,1:T(8,128)(2,1)S(1)}, u32[]{:S(2)}, u32[]{:S(2)}) collective-permute-start(bf16[32,1,8,128]{3,0,2,1:T(8,128)(2,1)S(1)} %get-tuple-element.57), channel_id=1, source_target_pairs={{0,8},{8,16},{16,24},{24,0},{1,9},{9,17},{17,25},{25,1},{2,10},{10... | collective-permute-start | bytes 196616 | tf_op jit(solution)/shard_map/ppermute | solution.py:14
  5.1 4.7 %collective-permute-start.1 = (bf16[32,1,8,128]{3,0,2,1:T(8,128)(2,1)S(1)}, bf16[32,1,8,128]{3,0,2,1:T(8,128)(2,1)S(1)}, u32[]{:S(2)}, u32[]{:S(2)}) collective-permute-start(bf16[32,1,8,128]{3,0,2,1:T(8,128)(2,1)S(1)} %get-tuple-element.56), channel_id=1, source_target_pairs={{8,0},{16,8},{24,16},{0,24},{9,1},{17,9},{25,17},{1,25},{10,2},{18... | collective-permute-start | bytes 196616 | tf_op jit(solution)/shard_map/ppermute | solution.py:16
  9.9 4.3 %collective-permute-start.3 = (bf16[32,10,1,128]{3,0,2,1:T(8,128)(2,1)S(1)}, bf16[32,10,1,128]{3,0,2,1:T(8,128)(2,1)S(1)}, u32[]{:S(2)}, u32[]{:S(2)}) collective-permute-start(bf16[32,10,1,128]{3,0,2,1:T(8,128)(2,1)S(1)} %get-tuple-element.52), channel_id=1, source_target_pairs={{1,0},{2,1},{3,2},{4,3},{5,4},{6,5},{7,6},{0,7},{9,8},{10,9},{11,1... | collective-permute-start | bytes 245768 | tf_op jit(solution)/shard_map/ppermute | solution.py:16
  12.1 5.7 %collective-permute-start.2 = (bf16[32,10,1,128]{3,0,2,1:T(8,128)(2,1)S(1)}, bf16[32,10,1,128]{3,0,2,1:T(8,128)(2,1)S(1)}, u32[]{:S(2)}, u32[]{:S(2)}) collective-permute-start(bf16[32,10,1,128]{3,0,2,1:T(8,128)(2,1)S(1)} %get-tuple-element.51), channel_id=1, source_target_pairs={{0,1},{1,2},{2,3},{3,4},{4,5},{5,6},{6,7},{7,0},{8,9},{9,10},{10,1... | collective-permute-start | bytes 245768 | tf_op jit(solution)/shard_map/ppermute | solution.py:14
  37.8 1.1 %copy-start.13 = (f32[32]{0:T(128)S(1)}, f32[32]{0:T(128)}, u32[]{:S(2)}) copy-start(f32[32]{0:T(128)} %param.9) | copy-start | bytes 388
  47.3 7.9 %copy-start.3 = (bf16[27,64,32]{1,2,0:T(8,128)(2,1)S(1)}, bf16[27,64,32]{1,2,0:T(8,128)(2,1)}, u32[]{:S(2)}) copy-start(bf16[27,64,32]{1,2,0:T(8,128)(2,1)} %param.10) | copy-start | bytes 331780
  47.4 4.4 %collective-permute-start.5 = (bf16[32,1,4,64]{0,3,2,1:T(8,128)(2,1)S(1)}, bf16[32,1,4,64]{0,3,2,1:T(8,128)(2,1)S(1)}, u32[]{:S(2)}, u32[]{:S(2)}) collective-permute-start(bf16[32,1,4,64]{0,3,2,1:T(8,128)(2,1)S(1)} %get-tuple-element.99), channel_id=1, source_target_pairs={{8,0},{16,8},{24,16},{0,24},{9,1},{17,9},{25,17},{1,25},{10,2},{18... | collective-permute-start | bytes 49160 | tf_op jit(solution)/shard_map/ppermute | solution.py:16
  49.5 5.2 %collective-permute-start.4 = (bf16[32,1,4,64]{0,3,2,1:T(8,128)(2,1)S(1)}, bf16[32,1,4,64]{0,3,2,1:T(8,128)(2,1)S(1)}, u32[]{:S(2)}, u32[]{:S(2)}) collective-permute-start(bf16[32,1,4,64]{0,3,2,1:T(8,128)(2,1)S(1)} %get-tuple-element.98), channel_id=1, source_target_pairs={{0,8},{8,16},{16,24},{24,0},{1,9},{9,17},{17,25},{25,1},{2,10},{10... | collective-permute-start | bytes 49160 | tf_op jit(solution)/shard_map/ppermute | solution.py:14
  54.7 3.1 %collective-permute-start.7 = (bf16[32,6,1,64]{0,3,2,1:T(8,128)(2,1)S(1)}, bf16[32,6,1,64]{0,3,2,1:T(8,128)(2,1)S(1)}, u32[]{:S(2)}, u32[]{:S(2)}) collective-permute-start(bf16[32,6,1,64]{0,3,2,1:T(8,128)(2,1)S(1)} %get-tuple-element.76), channel_id=1, source_target_pairs={{1,0},{2,1},{3,2},{4,3},{5,4},{6,5},{7,6},{0,7},{9,8},{10,9},{11,1... | collective-permute-start | bytes 73736 | tf_op jit(solution)/shard_map/ppermute | solution.py:16
  54.8 5.9 %collective-permute-start.6 = (bf16[32,6,1,64]{0,3,2,1:T(8,128)(2,1)S(1)}, bf16[32,6,1,64]{0,3,2,1:T(8,128)(2,1)S(1)}, u32[]{:S(2)}, u32[]{:S(2)}) collective-permute-start(bf16[32,6,1,64]{0,3,2,1:T(8,128)(2,1)S(1)} %get-tuple-element.75), channel_id=1, source_target_pairs={{0,1},{1,2},{2,3},{3,4},{4,5},{5,6},{6,7},{7,0},{8,9},{9,10},{10,1... | collective-permute-start | bytes 73736 | tf_op jit(solution)/shard_map/ppermute | solution.py:14
  66.2 0.8 copy-start.11
  67.0 17.6 %copy-start.1 = (bf16[27,128,64]{1,2,0:T(8,128)(2,1)S(1)}, bf16[27,128,64]{1,2,0:T(8,128)(2,1)}, u32[]{:S(2)}) copy-start(bf16[27,128,64]{1,2,0:T(8,128)(2,1)} %param.12) | copy-start | bytes 1327108
  84.5 6.1 %collective-permute-start.8 = (bf16[64,8,16,1]{0,2,3,1:T(8,128)(2,1)S(1)}, bf16[64,8,16,1]{0,2,3,1:T(8,128)(2,1)S(1)}, u32[]{:S(2)}, u32[]{:S(2)}) collective-permute-start(bf16[64,8,16,1]{0,2,3,1:T(8,128)(2,1)S(1)} %get-tuple-element.131), channel_id=1, source_target_pairs={{0,1},{1,2},{2,3},{3,4},{4,5},{5,6},{6,7},{7,0},{8,9},{9,10},{10,1... | collective-permute-start | bytes 49160 | tf_op jit(solution)/shard_map/ppermute | solution.py:14
  87.1 5.1 %collective-permute-start.9 = (bf16[64,8,16,1]{0,2,3,1:T(8,128)(2,1)S(1)}, bf16[64,8,16,1]{0,2,3,1:T(8,128)(2,1)S(1)}, u32[]{:S(2)}, u32[]{:S(2)}) collective-permute-start(bf16[64,8,16,1]{0,2,3,1:T(8,128)(2,1)S(1)} %get-tuple-element.130), channel_id=1, source_target_pairs={{1,0},{2,1},{3,2},{4,3},{5,4},{6,5},{7,6},{0,7},{9,8},{10,9},{11,1... | collective-permute-start | bytes 49160 | tf_op jit(solution)/shard_map/ppermute | solution.py:16
  92.2 0.6 copy-start.9
  94.2 0.9 copy-start.10
  96.3 1.0 copy-start.8
  96.5 1.0 %copy-start.7 = (bf16[3,128,64]{1,2,0:T(8,128)(2,1)S(1)}, bf16[3,128,64]{1,2,0:T(8,128)(2,1)}, u32[]{:S(2)}) copy-start(bf16[3,128,64]{1,2,0:T(8,128)(2,1)} %get-tuple-element.70) | copy-start | bytes 147460
  96.8 0.9 copy-start.6
  97.0 1.0 %copy-start.5 = (bf16[3,128,64]{1,2,0:T(8,128)(2,1)S(1)}, bf16[3,128,64]{1,2,0:T(8,128)(2,1)}, u32[]{:S(2)}) copy-start(bf16[3,128,64]{1,2,0:T(8,128)(2,1)} %get-tuple-element.68) | copy-start | bytes 147460
  97.3 0.9 copy-start.4
  98.2 0.9 copy-start.12
where the time goes:
time: 100 us
  local copies, waits for them, and re-layouts  21.7 us (22%)
  waiting for transfers between devices  19.9 us (20%)
  blocking collectives  16.5 us (16%)
  matrix products  14.8 us (15%)
  other arithmetic  12.9 us (13%)
  starting transfers between devices  12.6 us (13%)
  between operations  1.59 us (2%)
    dot_general x27, matrix products, convolve(): jnp.dot(mixing, stacked, preferred_element_type=jnp.float32)  14.8 us
    ppermute x5, waiting for transfers between devices, extended(): lax.ppermute(tail, axis, [(i, (i + 1) % count) for i in range(count)])  11.6 us
    ppermute x5, starting transfers between devices, extended(): lax.ppermute(head, axis, [((i + 1) % count, i) for i in range(count)])  8.9 us
    all_gather x1, blocking collectives, shards(): slab_rows = lax.all_gather(pieces, 'gx', axis=1, tiled=True)  8.49 us
    ppermute x5, waiting for transfers between devices, extended(): lax.ppermute(head, axis, [((i + 1) % count, i) for i in range(count)])  8.26 us
    all_to_all x1, blocking collectives, shards(): lax.all_to_all(coarse, 'gy', split_axis=3, concat_axis=2, tiled=True)  8.02 us
    concatenate x18, local copies, waits for them, and re-layouts, convolve(): jnp.concatenate([padded[:, offset_x:offset_x + extent_x, offset_y:offset_...  6.73 us
    reduce_sum x2, other arithmetic, average_pool(): return blocks.mean(axis=(2, 4, 6)).astype(jnp.bfloat16)  5.15 us
  transfers between devices with their start and end apart: 10, of which 9 were waited for; matrix products, arithmetic and copies ran while one was open for 4% of the time, Pallas kernels for 0%

commit v1 on v0

--- a/solution.py
+++ b/solution.py
@@ -74,7 +74,10 @@
     rimmed_three = extended(pooled, (("gx", 1), ("gy", 2)), 1)
     level_three = convolve(wrap_axis(rimmed_three, 3), weight_three, bias_three)
     coarse = average_pool(level_three)
-    pieces = lax.all_to_all(coarse, "gy", split_axis=3, concat_axis=2, tiled=True)
+    pieces = jnp.concatenate(
+        lax.all_to_all(jnp.stack(jnp.split(coarse, lax.axis_size("gy"), axis=3)), "gy", 0, 0),
+        axis=2,
+    )
     slab_rows = lax.all_gather(pieces, "gx", axis=1, tiled=True)
     deepened = extended(slab_rows, (("gy", 3),), 1)
     padded = wrap_axis(wrap_axis(deepened, 1), 2)

time: 100 us -> 100 us (level)
    unnamed x36 -> x43, local copies, waits for them, and re-layouts: 3.16 us -> 3.24 us
where the time goes in v1:
time: 100 us
  local copies, waits for them, and re-layouts  21.8 us (22%)
  waiting for transfers between devices  19.9 us (20%)
  blocking collectives  16.5 us (16%)
  matrix products  14.8 us (15%)
  other arithmetic  12.9 us (13%)
  starting transfers between devices  12.6 us (13%)
  between operations  1.62 us (2%)
    dot_general x27, matrix products, convolve(): jnp.dot(mixing, stacked, preferred_element_type=jnp.float32)  14.8 us
    ppermute x5, waiting for transfers between devices, extended(): lax.ppermute(tail, axis, [(i, (i + 1) % count) for i in range(count)])  11.6 us
    ppermute x5, starting transfers between devices, extended(): lax.ppermute(head, axis, [((i + 1) % count, i) for i in range(count)])  8.9 us
    all_gather x1, blocking collectives, shards(): slab_rows = lax.all_gather(pieces, 'gx', axis=1, tiled=True)  8.49 us
    ppermute x5, waiting for transfers between devices, extended(): lax.ppermute(head, axis, [((i + 1) % count, i) for i in range(count)])  8.26 us
    all_to_all x1, blocking collectives, shards(): lax.all_to_all(jnp.stack(jnp.split(coarse, lax.axis_size('gy'), axis=3)),...  8.02 us
    concatenate x18, local copies, waits for them, and re-layouts, convolve(): jnp.concatenate([padded[:, offset_x:offset_x + extent_x, offset_y:offset_...  6.73 us
    reduce_sum x2, other arithmetic, average_pool(): return blocks.mean(axis=(2, 4, 6)).astype(jnp.bfloat16)  5.15 us
  transfers between devices with their start and end apart: 10, of which 9 were waited for; matrix products, arithmetic and copies ran while one was open for 4% of the time, Pallas kernels for 0%

profile of v1, /device:TPU:0, one launch (start us, length us, event | category | flops | bytes accessed | tf_op | source)
XLA Modules:
  0.0 100.2 jit_solution(5755542956501353951)
XLA Ops:
  0.6 1.5 %copy.179 = bf16[32,8,8,128]{3,0,2,1:T(8,128)(2,1)S(1)} copy(bf16[32,8,8,128]{3,2,1,0:T(8,128)(2,1)} %param.7) | data formatting | bytes 1048576 | tf_op args[0]
  2.1 3.0 %collective-permute-start = (bf16[32,1,8,128]{3,0,2,1:T(8,128)(2,1)S(1)}, bf16[32,1,8,128]{3,0,2,1:T(8,128)(2,1)S(1)}, u32[]{:S(2)}, u32[]{:S(2)}) collective-permute-start(bf16[32,1,8,128]{3,0,2,1:T(8,128)(2,1)S(1)} %get-tuple-element.57), channel_id=1, source_target_pairs={{0,8},{8,16},{16,24},{24,0},{1,9},{9,17},{17,25},{25,1},{2,10},{10... | collective-permute-start | bytes 196616 | tf_op jit(solution)/shard_map/ppermute | solution.py:14
  5.1 1.0 %collective-permute-start.1 = (bf16[32,1,8,128]{3,0,2,1:T(8,128)(2,1)S(1)}, bf16[32,1,8,128]{3,0,2,1:T(8,128)(2,1)S(1)}, u32[]{:S(2)}, u32[]{:S(2)}) collective-permute-start(bf16[32,1,8,128]{3,0,2,1:T(8,128)(2,1)S(1)} %get-tuple-element.56), channel_id=1, source_target_pairs={{8,0},{16,8},{24,16},{0,24},{9,1},{17,9},{25,17},{1,25},{10,2},{18... | collective-permute-start | bytes 196616 | tf_op jit(solution)/shard_map/ppermute | solution.py:16
  6.2 2.3 %collective-permute-done = bf16[32,1,8,128]{3,0,2,1:T(8,128)(2,1)S(1)} collective-permute-done((bf16[32,1,8,128]{3,0,2,1:T(8,128)(2,1)S(1)}, bf16[32,1,8,128]{3,0,2,1:T(8,128)(2,1)S(1)}, u32[]{:S(2)}, u32[]{:S(2)}) %collective-permute-start) | collective-permute-done | bytes 65568 | tf_op jit(solution)/shard_map/ppermute | solution.py:14
  8.8 1.0 %collective-permute-done.1 = bf16[32,1,8,128]{3,0,2,1:T(8,128)(2,1)S(1)} collective-permute-done((bf16[32,1,8,128]{3,0,2,1:T(8,128)(2,1)S(1)}, bf16[32,1,8,128]{3,0,2,1:T(8,128)(2,1)S(1)}, u32[]{:S(2)}, u32[]{:S(2)}) %collective-permute-start.1) | collective-permute-done | bytes 65568 | tf_op jit(solution)/shard_map/ppermute | solution.py:16
  9.9 2.2 %collective-permute-start.3 = (bf16[32,10,1,128]{3,0,2,1:T(8,128)(2,1)S(1)}, bf16[32,10,1,128]{3,0,2,1:T(8,128)(2,1)S(1)}, u32[]{:S(2)}, u32[]{:S(2)}) collective-permute-start(bf16[32,10,1,128]{3,0,2,1:T(8,128)(2,1)S(1)} %get-tuple-element.52), channel_id=1, source_target_pairs={{1,0},{2,1},{3,2},{4,3},{5,4},{6,5},{7,6},{0,7},{9,8},{10,9},{11,1... | collective-permute-start | bytes 245768 | tf_op jit(solution)/shard_map/ppermute | solution.py:16
  13.2 1.0 %collective-permute-done.3 = bf16[32,10,1,128]{3,0,2,1:T(8,128)(2,1)S(1)} collective-permute-done((bf16[32,10,1,128]{3,0,2,1:T(8,128)(2,1)S(1)}, bf16[32,10,1,128]{3,0,2,1:T(8,128)(2,1)S(1)}, u32[]{:S(2)}, u32[]{:S(2)}) %collective-permute-start.3) | collective-permute-done | bytes 81952 | tf_op jit(solution)/shard_map/ppermute | solution.py:16
  14.2 3.6 %collective-permute-done.2 = bf16[32,10,1,128]{3,0,2,1:T(8,128)(2,1)S(1)} collective-permute-done((bf16[32,10,1,128]{3,0,2,1:T(8,128)(2,1)S(1)}, bf16[32,10,1,128]{3,0,2,1:T(8,128)(2,1)S(1)}, u32[]{:S(2)}, u32[]{:S(2)}) %collective-permute-start.2) | collective-permute-done | bytes 81952 | tf_op jit(solution)/shard_map/ppermute | solution.py:14
  18.2 1.7 %maximum_maximum_fusion = (bf16[32,10,10,129]{3,0,2,1:T(8,128)(2,1)S(1)}, bf16[32,10,10,129]{3,0,2,1:T(8,128)(2,1)S(1)}) fusion(bf16[32,10,1,128]{3,0,2,1:T(8,128)(2,1)S(1)} %collective-permute-done.3, bf16[32,10,8,128]{3,0,2,1:T(8,128)(2,1)S(1)} %constant_dynamic-update-slice_fusion, bf16[32,10,1,128]{3,0,2,1:T(8,128)(2,1)S(1)} %collective-permute-done.2, ...), kind=kLoop, calls=%fused_computation.11 | loop fusion | flops 6604800 | bytes 2483200 | tf_op jit(solution)/shard_map/concatenate | solution.py:26
  19.9 2.8 %fusion.60 = (bf16[32,8,8,128]{3,0,2,1:T(8,128)(2,1)S(1)}, bf16[32,8,8,128]{3,0,2,1:T(8,128)(2,1)S(1)}, bf16[32,8,8,128]{3,0,2,1:T(8,128)(2,1)S(1)}, bf16[32,8,8...) fusion(bf16[32,10,10,129]{3,0,2,1:T(8,128)(2,1)S(1)} %get-tuple, ...), kind=kLoop, calls=%fused_computation.180 | loop fusion | bytes 18874368 | tf_op jit(solution)/shard_map/slice | solution.py:40
  30.0 1.1 %fusion.18 = f32[8192,32]{0,1:T(8,128)S(1)} fusion(bf16[32,96]{1,0:T(8,128)(2,1)S(1)} %reshape.195, bf16[12,8,64,128]{3,2,1,0:T(8,128)(2,1)S(1)} %bitcast.258), kind=kOutput, calls=%fused_computation.29 | convolution fusion | flops 50331648 | bytes 2627584 | tf_op jit(solution)/shard_map/dot_general | solution.py:56
  31.1 1.1 %convolution_add_fusion.7 = f32[8192,32]{0,1:T(8,128)S(1)} fusion(f32[8192,32]{0,1:T(8,128)S(1)} %fusion.18, bf16[32,96]{1,0:T(8,128)(2,1)S(1)} %reshape.197, bf16[12,8,64,128]{3,2,1,0:T(8,128)(2,1)S(1)} %bitcast.259), kind=kOutput, calls=%fused_computation.9 | convolution fusion | flops 50593792 | bytes 3676160 | tf_op jit(solution)/shard_map/dot_general | solution.py:56
  32.2 1.1 %convolution_add_fusion.6 = f32[8192,32]{0,1:T(8,128)S(1)} fusion(f32[8192,32]{0,1:T(8,128)S(1)} %convolution_add_fusion.7, bf16[32,96]{1,0:T(8,128)(2,1)S(1)} %reshape.199, bf16[12,8,64,128]{3,2,1,0:T(8,128)(2,1)S(1)} %bitcast.260), kind=kOutput, calls=%fused_computation.8 | convolution fusion | flops 50593792 | bytes 3676160 | tf_op jit(solution)/shard_map/dot_general | solution.py:56
  33.4 1.1 %convolution_add_fusion.5 = f32[8192,32]{0,1:T(8,128)S(1)} fusion(f32[8192,32]{0,1:T(8,128)S(1)} %convolution_add_fusion.6, bf16[32,96]{1,0:T(8,128)(2,1)S(1)} %reshape.201, bf16[12,8,64,128]{3,2,1,0:T(8,128)(2,1)S(1)} %bitcast.262), kind=kOutput, calls=%fused_computation.7 | convolution fusion | flops 50593792 | bytes 3676160 | tf_op jit(solution)/shard_map/dot_general | solution.py:56
  34.5 1.1 %convolution_add_fusion.4 = f32[8192,32]{0,1:T(8,128)S(1)} fusion(f32[8192,32]{0,1:T(8,128)S(1)} %convolution_add_fusion.5, bf16[32,96]{1,0:T(8,128)(2,1)S(1)} %reshape.203, bf16[12,8,64,128]{3,2,1,0:T(8,128)(2,1)S(1)} %bitcast.261), kind=kOutput, calls=%fused_computation.6 | convolution fusion | flops 50593792 | bytes 3676160 | tf_op jit(solution)/shard_map/dot_general | solution.py:56
  35.6 1.1 %convolution_add_fusion.3 = f32[8192,32]{0,1:T(8,128)S(1)} fusion(f32[8192,32]{0,1:T(8,128)S(1)} %convolution_add_fusion.4, bf16[32,96]{1,0:T(8,128)(2,1)S(1)} %reshape.205, bf16[12,8,64,128]{3,2,1,0:T(8,128)(2,1)S(1)} %bitcast.263), kind=kOutput, calls=%fused_computation.5 | convolution fusion | flops 50593792 | bytes 3676160 | tf_op jit(solution)/shard_map/dot_general | solution.py:56
  36.7 1.1 %convolution_add_fusion.2 = f32[8192,32]{0,1:T(8,128)S(1)} fusion(f32[8192,32]{0,1:T(8,128)S(1)} %convolution_add_fusion.3, bf16[32,96]{1,0:T(8,128)(2,1)S(1)} %reshape.207, bf16[12,8,64,128]{3,2,1,0:T(8,128)(2,1)S(1)} %bitcast.265), kind=kOutput, calls=%fused_computation.4 | convolution fusion | flops 50593792 | bytes 3676160 | tf_op jit(solution)/shard_map/dot_general | solution.py:56
  37.9 1.1 %convolution_add_fusion.1 = f32[8192,32]{0,1:T(8,128)S(1)} fusion(f32[8192,32]{0,1:T(8,128)S(1)} %convolution_add_fusion.2, bf16[32,96]{1,0:T(8,128)(2,1)S(1)} %reshape.209, bf16[12,8,64,128]{3,2,1,0:T(8,128)(2,1)S(1)} %bitcast.264), kind=kOutput, calls=%fused_computation.3 | convolution fusion | flops 50593792 | bytes 3676160 | tf_op jit(solution)/shard_map/dot_general | solution.py:56
  39.0 1.1 %fusion.31 = bf16[32,8192]{1,0:T(8,128)(2,1)S(1)} fusion(f32[8192,32]{0,1:T(8,128)S(1)} %convolution_add_fusion.1, bf16[32,96]{1,0:T(8,128)(2,1)S(1)} %reshape.211, bf16[12,8,64,128]{3,2,1,0:T(8,128)(2,1)S(1)} %bitcast.266, f32[32]{0:T(128)S(1)} %copy-done.13), kind=kOutput, calls=%fused_computation.49 | convolution fusion | flops 51904512 | bytes 3152000 | tf_op jit(solution)/shard_map/dot_general | solution.py:56
  40.1 2.4 %copy.203 = f32[32,8192]{0,1:T(8,128)} copy(bf16[32,8192]{1,0:T(8,128)(2,1)S(1)} %fusion.31) | data formatting | bytes 1572864 | tf_op jit(solution)/shard_map/convert_element_type | solution.py:64
  42.5 4.8 %reduce_sum.18 = f32[32,4,4,64]{0,3,2,1:T(8,128)S(1)} reduce(f32[32,4,2,4,2,64,2]{0,6,5,4,3,2,1:T(2,128)} %bitcast.257, f32[]{:T(128)} %constant.6.clone.1), dimensions={2,4,6}, to_apply=%region_0.1 | reduce | flops 229376 | bytes 1179652 | tf_op jit(solution)/shard_map/reduce_sum | solution.py:67
  47.4 2.1 %collective-permute-start.5 = (bf16[32,1,4,64]{0,3,2,1:T(8,128)(2,1)S(1)}, bf16[32,1,4,64]{0,3,2,1:T(8,128)(2,1)S(1)}, u32[]{:S(2)}, u32[]{:S(2)}) collective-permute-start(bf16[32,1,4,64]{0,3,2,1:T(8,128)(2,1)S(1)} %get-tuple-element.99), channel_id=1, source_target_pairs={{8,0},{16,8},{24,16},{0,24},{9,1},{17,9},{25,17},{1,25},{10,2},{18... | collective-permute-start | bytes 49160 | tf_op jit(solution)/shard_map/ppermute | solution.py:16
  49.6 2.2 %collective-permute-done.5 = bf16[32,1,4,64]{0,3,2,1:T(8,128)(2,1)S(1)} collective-permute-done((bf16[32,1,4,64]{0,3,2,1:T(8,128)(2,1)S(1)}, bf16[32,1,4,64]{0,3,2,1:T(8,128)(2,1)S(1)}, u32[]{:S(2)}, u32[]{:S(2)}) %collective-permute-start.5) | collective-permute-done | bytes 16416 | tf_op jit(solution)/shard_map/ppermute | solution.py:16
  51.8 2.9 %collective-permute-done.4 = bf16[32,1,4,64]{0,3,2,1:T(8,128)(2,1)S(1)} collective-permute-done((bf16[32,1,4,64]{0,3,2,1:T(8,128)(2,1)S(1)}, bf16[32,1,4,64]{0,3,2,1:T(8,128)(2,1)S(1)}, u32[]{:S(2)}, u32[]{:S(2)}) %collective-permute-start.4) | collective-permute-done | bytes 16416 | tf_op jit(solution)/shard_map/ppermute | solution.py:14
  55.3 2.5 %collective-permute-done.7 = bf16[32,6,1,64]{0,3,2,1:T(8,128)(2,1)S(1)} collective-permute-done((bf16[32,6,1,64]{0,3,2,1:T(8,128)(2,1)S(1)}, bf16[32,6,1,64]{0,3,2,1:T(8,128)(2,1)S(1)}, u32[]{:S(2)}, u32[]{:S(2)}) %collective-permute-start.7) | collective-permute-done | bytes 24608 | tf_op jit(solution)/shard_map/ppermute | solution.py:16
  57.8 2.9 %collective-permute-done.6 = bf16[32,6,1,64]{0,3,2,1:T(8,128)(2,1)S(1)} collective-permute-done((bf16[32,6,1,64]{0,3,2,1:T(8,128)(2,1)S(1)}, bf16[32,6,1,64]{0,3,2,1:T(8,128)(2,1)S(1)}, u32[]{:S(2)}, u32[]{:S(2)}) %collective-permute-start.6) | collective-permute-done | bytes 24608 | tf_op jit(solution)/shard_map/ppermute | solution.py:14
  68.0 8.0 %all_to_all.5 = bf16[8,2,512]{2,1,0:T(2,128)(2,1)S(1)} all-to-all(bf16[8,2,512]{2,1,0:T(2,128)(2,1)S(1)} %reshape.255), channel_id=1, replica_groups=mesh['gx'=4,'gy'=8] {'gy'}, dimensions={0} | all-to-all | bytes 32768 | tf_op jit(solution)/shard_map/all_to_all | solution.py:78
  76.2 8.5 %all_gather.3 = bf16[64,8,16,4]{0,2,3,1:T(8,128)(2,1)S(1)} all-gather(bf16[64,2,16,4]{0,2,3,1:T(8,128)(2,1)S(1)} %bitcast.289), channel_id=1, replica_groups=mesh['gx'=4,'gy'=8] {'gx'}, dimensions={1}, use_global_device_ids=true | all-gather | bytes 81920 | tf_op jit(solution)/shard_map/all_gather | solution.py:81
  85.4 0.9 copy.225
  86.4 0.9 reshape.231
  87.2 3.5 %collective-permute-start.9 = (bf16[64,8,16,1]{0,2,3,1:T(8,128)(2,1)S(1)}, bf16[64,8,16,1]{0,2,3,1:T(8,128)(2,1)S(1)}, u32[]{:S(2)}, u32[]{:S(2)}) collective-permute-start(bf16[64,8,16,1]{0,2,3,1:T(8,128)(2,1)S(1)} %get-tuple-element.130), channel_id=1, source_target_pairs={{1,0},{2,1},{3,2},{4,3},{5,4},{6,5},{7,6},{0,7},{9,8},{10,9},{11,1... | collective-permute-start | bytes 49160 | tf_op jit(solution)/shard_map/ppermute | solution.py:16
  90.8 1.6 %collective-permute-done.9 = bf16[64,8,16,1]{0,2,3,1:T(8,128)(2,1)S(1)} collective-permute-done((bf16[64,8,16,1]{0,2,3,1:T(8,128)(2,1)S(1)}, bf16[64,8,16,1]{0,2,3,1:T(8,128)(2,1)S(1)}, u32[]{:S(2)}, u32[]{:S(2)}) %collective-permute-start.9) | collective-permute-done | bytes 16416 | tf_op jit(solution)/shard_map/ppermute | solution.py:16
  (164 shorter events, 25.3 us)
Async XLA Ops:
  0.6 7.8 %copy-start = (bf16[32,8,8,128]{3,2,1,0:T(8,128)(2,1)S(1)}, bf16[32,8,8,128]{3,2,1,0:T(8,128)(2,1)}, u32[]{:S(2)}) copy-start(bf16[32,8,8,128]{3,2,1,0:T(8,128)(2,1)} %param.7) | copy-start | bytes 1572868
  0.6 11.5 %copy-start.2 = (bf16[27,32,32]{2,1,0:T(8,128)(2,1)S(1)}, bf16[27,32,32]{2,1,0:T(8,128)(2,1)}, u32[]{:S(2)}) copy-start(bf16[27,32,32]{2,1,0:T(8,128)(2,1)} %param.8) | copy-start | bytes 165892
  2.1 6.3 %collective-permute-start = (bf16[32,1,8,128]{3,0,2,1:T(8,128)(2,1)S(1)}, bf16[32,1,8,128]{3,0,2,1:T(8,128)(2,1)S(1)}, u32[]{:S(2)}, u32[]{:S(2)}) collective-permute-start(bf16[32,1,8,128]{3,0,2,1:T(8,128)(2,1)S(1)} %get-tuple-element.57), channel_id=1, source_target_pairs={{0,8},{8,16},{16,24},{24,0},{1,9},{9,17},{17,25},{25,1},{2,10},{10... | collective-permute-start | bytes 196616 | tf_op jit(solution)/shard_map/ppermute | solution.py:14
  5.1 4.7 %collective-permute-start.1 = (bf16[32,1,8,128]{3,0,2,1:T(8,128)(2,1)S(1)}, bf16[32,1,8,128]{3,0,2,1:T(8,128)(2,1)S(1)}, u32[]{:S(2)}, u32[]{:S(2)}) collective-permute-start(bf16[32,1,8,128]{3,0,2,1:T(8,128)(2,1)S(1)} %get-tuple-element.56), channel_id=1, source_target_pairs={{8,0},{16,8},{24,16},{0,24},{9,1},{17,9},{25,17},{1,25},{10,2},{18... | collective-permute-start | bytes 196616 | tf_op jit(solution)/shard_map/ppermute | solution.py:16
  9.9 4.3 %collective-permute-start.3 = (bf16[32,10,1,128]{3,0,2,1:T(8,128)(2,1)S(1)}, bf16[32,10,1,128]{3,0,2,1:T(8,128)(2,1)S(1)}, u32[]{:S(2)}, u32[]{:S(2)}) collective-permute-start(bf16[32,10,1,128]{3,0,2,1:T(8,128)(2,1)S(1)} %get-tuple-element.52), channel_id=1, source_target_pairs={{1,0},{2,1},{3,2},{4,3},{5,4},{6,5},{7,6},{0,7},{9,8},{10,9},{11,1... | collective-permute-start | bytes 245768 | tf_op jit(solution)/shard_map/ppermute | solution.py:16
  12.1 5.7 %collective-permute-start.2 = (bf16[32,10,1,128]{3,0,2,1:T(8,128)(2,1)S(1)}, bf16[32,10,1,128]{3,0,2,1:T(8,128)(2,1)S(1)}, u32[]{:S(2)}, u32[]{:S(2)}) collective-permute-start(bf16[32,10,1,128]{3,0,2,1:T(8,128)(2,1)S(1)} %get-tuple-element.51), channel_id=1, source_target_pairs={{0,1},{1,2},{2,3},{3,4},{4,5},{5,6},{6,7},{7,0},{8,9},{9,10},{10,1... | collective-permute-start | bytes 245768 | tf_op jit(solution)/shard_map/ppermute | solution.py:14
  37.8 1.1 %copy-start.13 = (f32[32]{0:T(128)S(1)}, f32[32]{0:T(128)}, u32[]{:S(2)}) copy-start(f32[32]{0:T(128)} %param.9) | copy-start | bytes 388
  47.3 7.9 %copy-start.3 = (bf16[27,64,32]{1,2,0:T(8,128)(2,1)S(1)}, bf16[27,64,32]{1,2,0:T(8,128)(2,1)}, u32[]{:S(2)}) copy-start(bf16[27,64,32]{1,2,0:T(8,128)(2,1)} %param.10) | copy-start | bytes 331780
  47.4 4.4 %collective-permute-start.5 = (bf16[32,1,4,64]{0,3,2,1:T(8,128)(2,1)S(1)}, bf16[32,1,4,64]{0,3,2,1:T(8,128)(2,1)S(1)}, u32[]{:S(2)}, u32[]{:S(2)}) collective-permute-start(bf16[32,1,4,64]{0,3,2,1:T(8,128)(2,1)S(1)} %get-tuple-element.99), channel_id=1, source_target_pairs={{8,0},{16,8},{24,16},{0,24},{9,1},{17,9},{25,17},{1,25},{10,2},{18... | collective-permute-start | bytes 49160 | tf_op jit(solution)/shard_map/ppermute | solution.py:16
  49.5 5.2 %collective-permute-start.4 = (bf16[32,1,4,64]{0,3,2,1:T(8,128)(2,1)S(1)}, bf16[32,1,4,64]{0,3,2,1:T(8,128)(2,1)S(1)}, u32[]{:S(2)}, u32[]{:S(2)}) collective-permute-start(bf16[32,1,4,64]{0,3,2,1:T(8,128)(2,1)S(1)} %get-tuple-element.98), channel_id=1, source_target_pairs={{0,8},{8,16},{16,24},{24,0},{1,9},{9,17},{17,25},{25,1},{2,10},{10... | collective-permute-start | bytes 49160 | tf_op jit(solution)/shard_map/ppermute | solution.py:14
  54.7 3.1 %collective-permute-start.7 = (bf16[32,6,1,64]{0,3,2,1:T(8,128)(2,1)S(1)}, bf16[32,6,1,64]{0,3,2,1:T(8,128)(2,1)S(1)}, u32[]{:S(2)}, u32[]{:S(2)}) collective-permute-start(bf16[32,6,1,64]{0,3,2,1:T(8,128)(2,1)S(1)} %get-tuple-element.76), channel_id=1, source_target_pairs={{1,0},{2,1},{3,2},{4,3},{5,4},{6,5},{7,6},{0,7},{9,8},{10,9},{11,1... | collective-permute-start | bytes 73736 | tf_op jit(solution)/shard_map/ppermute | solution.py:16
  54.8 5.9 %collective-permute-start.6 = (bf16[32,6,1,64]{0,3,2,1:T(8,128)(2,1)S(1)}, bf16[32,6,1,64]{0,3,2,1:T(8,128)(2,1)S(1)}, u32[]{:S(2)}, u32[]{:S(2)}) collective-permute-start(bf16[32,6,1,64]{0,3,2,1:T(8,128)(2,1)S(1)} %get-tuple-element.75), channel_id=1, source_target_pairs={{0,1},{1,2},{2,3},{3,4},{4,5},{5,6},{6,7},{7,0},{8,9},{9,10},{10,1... | collective-permute-start | bytes 73736 | tf_op jit(solution)/shard_map/ppermute | solution.py:14
  66.2 0.8 copy-start.11
  67.0 17.8 %copy-start.1 = (bf16[27,128,64]{1,2,0:T(8,128)(2,1)S(1)}, bf16[27,128,64]{1,2,0:T(8,128)(2,1)}, u32[]{:S(2)}) copy-start(bf16[27,128,64]{1,2,0:T(8,128)(2,1)} %param.12) | copy-start | bytes 1327108
  84.7 6.1 %collective-permute-start.8 = (bf16[64,8,16,1]{0,2,3,1:T(8,128)(2,1)S(1)}, bf16[64,8,16,1]{0,2,3,1:T(8,128)(2,1)S(1)}, u32[]{:S(2)}, u32[]{:S(2)}) collective-permute-start(bf16[64,8,16,1]{0,2,3,1:T(8,128)(2,1)S(1)} %get-tuple-element.131), channel_id=1, source_target_pairs={{0,1},{1,2},{2,3},{3,4},{4,5},{5,6},{6,7},{7,0},{8,9},{9,10},{10,1... | collective-permute-start | bytes 49160 | tf_op jit(solution)/shard_map/ppermute | solution.py:14
  87.2 5.1 %collective-permute-start.9 = (bf16[64,8,16,1]{0,2,3,1:T(8,128)(2,1)S(1)}, bf16[64,8,16,1]{0,2,3,1:T(8,128)(2,1)S(1)}, u32[]{:S(2)}, u32[]{:S(2)}) collective-permute-start(bf16[64,8,16,1]{0,2,3,1:T(8,128)(2,1)S(1)} %get-tuple-element.130), channel_id=1, source_target_pairs={{1,0},{2,1},{3,2},{4,3},{5,4},{6,5},{7,6},{0,7},{9,8},{10,9},{11,1... | collective-permute-start | bytes 49160 | tf_op jit(solution)/shard_map/ppermute | solution.py:16
  92.4 0.6 copy-start.9
  94.3 0.9 copy-start.10
  96.5 1.0 copy-start.8
  96.7 1.0 %copy-start.7 = (bf16[3,128,64]{1,2,0:T(8,128)(2,1)S(1)}, bf16[3,128,64]{1,2,0:T(8,128)(2,1)}, u32[]{:S(2)}) copy-start(bf16[3,128,64]{1,2,0:T(8,128)(2,1)} %get-tuple-element.70) | copy-start | bytes 147460
  97.0 1.0 copy-start.6
  97.1 1.0 %copy-start.5 = (bf16[3,128,64]{1,2,0:T(8,128)(2,1)S(1)}, bf16[3,128,64]{1,2,0:T(8,128)(2,1)}, u32[]{:S(2)}) copy-start(bf16[3,128,64]{1,2,0:T(8,128)(2,1)} %get-tuple-element.68) | copy-start | bytes 147460
  97.5 0.9 copy-start.4
  98.4 0.9 copy-start.12
